TPU v7x, 32 devices: a whole 2x2x4 slice. The times are simulated.
32 devices in a mesh: grp: 2 (over x), lat: 16 (over z, y, core).
Axes of the slice: x: 2, y: 2, z: 4, core: 2. Of those that a mesh axis runs over, the one named last changes fastest.
Arguments:
- acts: bfloat16 [128, 2, 2048], P(('grp', 'lat')), parts along dimension 0, may hold values from -6 to 6
- enc_weight: bfloat16 [4, 2048, 4096], P('grp', None, 'lat'), parts along dimension 0, may hold values from -0.09375 to 0.09375
- enc_bias: float32 [8192], P(('grp', 'lat')), parts along dimension 0, may hold values from -3 to 3
- dec_weight: bfloat16 [4096, 4, 2048], P('lat', 'grp'), parts along dimension 1, may hold values from -0.125 to 0.125
- dec_bias: float32 [4, 2048], P('grp'), parts along dimension 0, may hold values from -5 to 5
Outputs:
- residual: bfloat16 [128, 2, 2048], P(('grp', 'lat')), parts along dimension 0
- grad_enc: bfloat16 [4, 2048, 4096], P('grp', None, 'lat'), parts along dimension 0
- grad_enc_bias: float32 [8192], P(('grp', 'lat')), parts along dimension 0
- grad_dec: bfloat16 [4096, 4, 2048], P('lat', 'grp'), parts along dimension 1
- grad_dec_bias: float32 [4, 2048], P('grp'), parts along dimension 0
There are 2 independent parts, one for each index of `grp`. A program takes and returns all parts, laid end to end along the dimension named above; each array names one. Nothing has to cross between parts.
All inputs are finite; a program needn't handle non-finite values.
Results may differ from a plain program's by a relative error of at most 0.015.
Values may be sent and summed in bfloat16 or wider, within the bound.
No kernel may reach another device: no remote copies, remote signals or barrier semaphores. Data moves between devices by JAX's collectives and lax.ppermute only.
A program may use at most 128 MiB of HBM per device.

v0:
```python
import jax
import jax.numpy as jnp
from jax import lax
from jax.sharding import PartitionSpec as P

sparsity_weight = 2.0


def body(acts, enc_weight, enc_bias, dec_weight, dec_bias):
    tok_dev, layers, width = acts.shape
    lat_dev = enc_weight.shape[2]
    wide = layers * width
    total_rows = tok_dev * lax.axis_size("lat")
    factor = 2.0 / total_rows
    flat_rows = acts.reshape(tok_dev, wide)
    flat_enc = enc_weight.reshape(wide, lat_dev)
    flat_dec = dec_weight.reshape(lat_dev, wide)
    flat_bias = dec_bias.reshape(wide)
    own_start = lax.axis_index("lat") * tok_dev
    gathered = lax.all_gather(flat_rows, "lat", axis=0, tiled=True)
    before = jnp.dot(gathered, flat_enc, preferred_element_type=jnp.float32) + enc_bias
    active = jnp.maximum(before, 0.0).astype(jnp.bfloat16)
    dec_wide = dec_weight.astype(jnp.float32)
    row_sq = jnp.sum(dec_wide * dec_wide, axis=2)
    inv_norm = lax.rsqrt(row_sq + 1.0)
    dec_norm = jnp.sum(jnp.sqrt(row_sq + 1.0), axis=1)
    term = jnp.dot(active, flat_dec, preferred_element_type=jnp.float32)
    own_term = lax.dynamic_slice_in_dim(term, own_start, tok_dev, 0)
    own_term = own_term + flat_bias - flat_rows.astype(jnp.float32)
    term = lax.dynamic_update_slice_in_dim(term, own_term, own_start, 0)
    summed = lax.psum(term, "lat")
    all_residual = summed.astype(jnp.bfloat16)
    own_residual = lax.dynamic_slice_in_dim(all_residual, own_start, tok_dev, 0)
    grad_dec_bias = factor * jnp.sum(all_residual.astype(jnp.float32), axis=0)
    dec_total = lax.dot_general(
        active, all_residual, (((0,), (0,)), ((), ())), preferred_element_type=jnp.float32
    )
    backward = lax.dot_general(
        all_residual, flat_dec, (((1,), (1,)), ((), ())), preferred_element_type=jnp.float32
    )
    grad_act = factor * backward + sparsity_weight / total_rows * dec_norm
    grad_before = jnp.where(before > 0.0, grad_act, 0.0).astype(jnp.bfloat16)
    enc_total = lax.dot_general(
        gathered, grad_before, (((0,), (0,)), ((), ())), preferred_element_type=jnp.float32
    )
    grad_enc = enc_total.astype(jnp.bfloat16).reshape(layers, width, lat_dev)
    grad_enc_bias = jnp.sum(grad_before.astype(jnp.float32), axis=0)
    act_sum = jnp.sum(active.astype(jnp.float32), axis=0)
    grad_dec = (
        factor * dec_total.reshape(lat_dev, layers, width)
        + sparsity_weight / total_rows * act_sum[:, None, None] * dec_wide * inv_norm[:, :, None]
    ).astype(jnp.bfloat16)
    return (
        own_residual.reshape(tok_dev, layers, width),
        grad_enc,
        grad_enc_bias,
        grad_dec,
        grad_dec_bias.reshape(layers, width),
    )


def solution(mesh):
    return jax.shard_map(
        body,
        mesh=mesh,
        in_specs=(
            P(("grp", "lat"), None, None),
            P("grp", None, "lat"),
            P(("grp", "lat")),
            P("lat", "grp", None),
            P("grp", None),
        ),
        out_specs=(
            P(("grp", "lat"), None, None),
            P("grp", None, "lat"),
            P(("grp", "lat")),
            P("lat", "grp", None),
            P("grp", None),
        ),
        check_vma=False,
    )
```

profile of v0, /device:TPU:0, one launch (start us, length us, event | category | flops | bytes accessed | tf_op | source)
XLA Modules:
  0.0 136.5 jit_solution(2590079693091624209)
XLA Ops:
  0.6 0.0 copy-start
  0.7 1.6 %copy-done = bf16[2,2048,256]{2,1,0:T(8,128)(2,1)S(1)} copy-done((bf16[2,2048,256]{2,1,0:T(8,128)(2,1)S(1)}, bf16[2,2048,256]{2,1,0:T(8,128)(2,1)}, u32[]{:S(2)}) %copy-start) | copy-done | bytes 2097176
  2.2 0.7 copy.14
  2.9 0.8 reshape.50
  3.7 0.8 convert_bitcast_fusion
  4.5 0.0 copy-start.3
  4.6 3.8 %fusion.1 = f32[256,2]{1,0:T(8,128)S(1)} fusion(bf16[256,2,2048]{2,1,0:T(2,128)(2,1)} %param.8), kind=kLoop, calls=%fused_computation.5 | loop fusion | flops 3145216 | bytes 2099200 | tf_op jit(solution)/shard_map/reduce_sum | solution.py:24
  8.4 0.1 add_rsqrt_fusion
  8.6 24.6 %all-gather = bf16[16,4,4096]{2,1,0:T(4,128)(2,1)S(1)} all-gather(bf16[1,4,4096]{2,1,0:T(4,128)(2,1)S(1)} %reshape.50), channel_id=1, replica_groups=mesh['grp'=2,'lat'=16] {'lat'}, dimensions={0}, use_global_device_ids=true | all-gather | bytes 557056 | tf_op jit(solution)/shard_map/all_gather | solution.py:20
  33.2 0.1 reshape.51
  33.3 0.0 copy-done.3
  33.3 0.0 copy-start.1
  33.3 0.5 convert_reduce_fusion.1
  33.8 1.1 copy-done.1
  34.9 0.9 copy.13
  35.8 0.0 copy-start.2
  35.8 1.3 copy-done.2
  37.1 1.5 %fusion.8 = f32[64,4096]{1,0:T(8,128)} fusion(bf16[256,4096]{1,0:T(8,128)(2,1)S(1)} %bitcast.21, f32[64,256]{1,0:T(8,128)S(1)} %get-tuple-element.20), kind=kOutput, calls=%fused_computation.26 | convolution fusion | flops 134250496 | bytes 3211264 | tf_op jit(solution)/shard_map/dot_general | solution.py:27
  38.6 1.6 %subtract_dynamic-update-slice_fusion = f32[64,4096]{1,0:T(8,128)} fusion(f32[64,4096]{1,0:T(8,128)} %fusion.8, s32[]{:T(128)S(6)} %select_n.9, f32[4,4096]{1,0:T(4,128)S(1)} %bitcast.24, f32[4096]{0:T(1024)S(1)} %bitcast.25), kind=kLoop, calls=%fused_computation.20 | loop fusion | flops 32768 | bytes 212996 | tf_op jit(solution)/shard_map/dynamic_update_slice | solution.py:30
  40.1 70.1 %all-reduce.1 = bf16[64,4096]{1,0:T(8,128)(2,1)S(1)} all-reduce(f32[64,4096]{1,0:T(8,128)} %subtract_dynamic-update-slice_fusion), channel_id=1, replica_groups=mesh['grp'=2,'lat'=16] {'lat'}, use_global_device_ids=true, to_apply=%region_0.0 | all-reduce | flops 262144 | bytes 1572864 | tf_op jit(solution)/shard_map/psum | solution.py:31
  110.2 2.9 %convert_reduce_fusion.2 = (f32[256]{0:T(256)}, bf16[64,256]{1,0:T(8,128)(2,1)S(1)}) fusion(f32[256]{0:T(256)S(1)} %broadcast_multiply_fusion.2, bf16[64,4096]{1,0:T(8,128)(2,1)S(1)} %all-reduce.1, bf16[256,4096]{1,0:T(8,128)(2,1)} %bitcast.22, f32[64,256]{1,0:T(8,128)S(1)} %get-tuple-element.20), kind=kOutput, calls=%fused_computation.19 | convolution fusion | flops 134332160 | bytes 2721792 | tf_op jit(solution)/shard_map/dot_general | solution.py:38
  113.1 0.1 convert_reduce_fusion
  113.3 0.6 mul.82
  113.9 0.7 reshape.48
  114.6 2.0 %fusion = bf16[4096,256]{0,1:T(8,128)(2,1)} fusion(bf16[64,256]{1,0:T(8,128)(2,1)S(1)} %get-tuple-element.18, bf16[64,4096]{1,0:T(8,128)(2,1)S(1)} %reshape.51), kind=kOutput, calls=%fused_computation.4 | convolution fusion | flops 135266304 | bytes 2654208 | tf_op jit(solution)/shard_map/dot_general | solution.py:43
  116.6 4.1 %copy.12 = bf16[4096,256]{1,0:T(8,128)(2,1)} copy(bf16[4096,256]{0,1:T(8,128)(2,1)} %fusion) | data formatting | bytes 4194304
  120.7 2.7 %convolution_multiply_fusion = f32[256,4096]{1,0:T(8,128)} fusion(bf16[64,4096]{1,0:T(8,128)(2,1)S(1)} %all-reduce.1, f32[64,256]{1,0:T(8,128)S(1)} %get-tuple-element.20), kind=kOutput, calls=%fused_computation | convolution fusion | flops 135299072 | bytes 4784128 | tf_op jit(solution)/shard_map/dot_general | solution.py:35
  123.3 6.6 %mul.74 = f32[256,2,2048]{2,1,0:T(2,128)} reshape(f32[256,4096]{1,0:T(8,128)} %convolution_multiply_fusion) | data formatting | bytes 8388608 | tf_op jit(solution)/shard_map/mul | solution.py:50
  129.9 6.7 %fusion.4 = bf16[256,2,2048]{2,1,0:T(2,128)(2,1)} fusion(f32[256,2,2048]{2,1,0:T(2,128)} %mul.74, bf16[256,2,2048]{2,1,0:T(2,128)(2,1)} %param.8, f32[256]{0:T(256)S(1)} %broadcast_multiply_fusion.1, f32[256,2]{1,0:T(8,128)S(1)} %get-tuple-element.15), kind=kLoop, calls=%fused_computation.8 | loop fusion | flops 5242880 | bytes 8391680 | tf_op jit(solution)/shard_map/convert_element_type | solution.py:52
  (5 shorter events, 0.1 us)
Async XLA Ops:
  0.6 1.6 %copy-start = (bf16[2,2048,256]{2,1,0:T(8,128)(2,1)S(1)}, bf16[2,2048,256]{2,1,0:T(8,128)(2,1)}, u32[]{:S(2)}) copy-start(bf16[2,2048,256]{2,1,0:T(8,128)(2,1)} %param.6) | copy-start | bytes 6291460
  4.5 28.8 %copy-start.3 = (f32[256]{0:T(256)S(1)}, f32[256]{0:T(256)}, u32[]{:S(2)}) copy-start(f32[256]{0:T(256)} %param.7) | copy-start | bytes 3076
  33.3 1.6 %copy-start.1 = (bf16[256,2,2048]{2,1,0:T(2,128)(2,1)S(1)}, bf16[256,2,2048]{2,1,0:T(2,128)(2,1)}, u32[]{:S(2)}) copy-start(bf16[256,2,2048]{2,1,0:T(2,128)(2,1)} %param.8) | copy-start | bytes 6291460
  35.8 1.3 copy-start.2
where the time goes:
time: 137 us
  blocking collectives  94.7 us (69%)
  local copies, waits for them, and re-layouts  18.5 us (14%)
  other arithmetic  13.1 us (10%)
  matrix products  9.56 us (7%)
    psum x1, blocking collectives, body(): summed = lax.psum(term, 'lat')  70.1 us
    all_gather x1, blocking collectives, body(): gathered = lax.all_gather(flat_rows, 'lat', axis=0, tiled=True)  24.6 us
    unnamed x14, local copies, waits for them, and re-layouts  10.6 us
    convert_element_type x1, other arithmetic, body(): grad_dec = (factor * dec_total.reshape(lat_dev, layers, width) + sparsity...  6.65 us
    mul x1, local copies, waits for them, and re-layouts, body(): factor * dec_total.reshape(lat_dev, layers, width)  6.57 us
    reduce_sum x1, other arithmetic, body(): row_sq = jnp.sum(dec_wide * dec_wide, axis=2)  3.84 us
    dot_general x1, matrix products, body(): lax.dot_general(all_residual, flat_dec, (((1,), (1,)), ((), ())), preferr...  2.94 us

commit v1 on v0

--- a/solution.py
+++ b/solution.py
@@ -28,7 +28,9 @@
     own_term = lax.dynamic_slice_in_dim(term, own_start, tok_dev, 0)
     own_term = own_term + flat_bias - flat_rows.astype(jnp.float32)
     term = lax.dynamic_update_slice_in_dim(term, own_term, own_start, 0)
-    summed = lax.psum(term, "lat")
+    summed = term
+    for hop in (1, 2, 4, 8):
+        summed = summed + lax.ppermute(summed, "lat", [(dev, dev ^ hop) for dev in range(16)])
     all_residual = summed.astype(jnp.bfloat16)
     own_residual = lax.dynamic_slice_in_dim(all_residual, own_start, tok_dev, 0)
     grad_dec_bias = factor * jnp.sum(all_residual.astype(jnp.float32), axis=0)

time: 137 us -> 159 us (1.16)
  waiting for transfers between devices: 0 us -> 96.9 us
  blocking collectives: 94.7 us -> 24.6 us
  other arithmetic: 13.1 us -> 10.4 us
  matrix products: 9.56 us -> 6.99 us
    ppermute x0 -> x4, waiting for transfers between devices: none -> 96.9 us  [body(): lax.ppermute(summed, 'lat', [(dev, dev ^ hop) for dev in range(16)])]
    psum x1 -> x0, blocking collectives: 70.1 us -> none  [body(): summed = lax.psum(term, 'lat')]
    reduce_sum x1, other arithmetic: 3.84 us -> 2.24 us  [body(): row_sq = jnp.sum(dec_wide * dec_wide, axis=2)]
    dot_general x1, matrix products: 2.94 us -> 1.34 us  [body(): lax.dot_general(all_residual, flat_dec, (((1,), (1,)), ((), ())), preferr...]
  transfers between devices with their start and end apart: 0 -> 4, of which waited for: 0 -> 4; matrix products, arithmetic and copies ran while one was open for 0% -> 1% of each run, Pallas kernels for 0% -> 0%
where the time goes in v1:
time: 159 us
  waiting for transfers between devices  96.9 us (61%)
  blocking collectives  24.6 us (15%)
  local copies, waits for them, and re-layouts  18.7 us (12%)
  other arithmetic  10.4 us (7%)
  matrix products  6.99 us (4%)
    ppermute x4, waiting for transfers between devices, body(): lax.ppermute(summed, 'lat', [(dev, dev ^ hop) for dev in range(16)])  96.9 us
    all_gather x1, blocking collectives, body(): gathered = lax.all_gather(flat_rows, 'lat', axis=0, tiled=True)  24.6 us
    unnamed x14, local copies, waits for them, and re-layouts  10.8 us
    convert_element_type x1, other arithmetic, body(): grad_dec = (factor * dec_total.reshape(lat_dev, layers, width) + sparsity...  6.65 us
    mul x1, local copies, waits for them, and re-layouts, body(): factor * dec_total.reshape(lat_dev, layers, width)  6.57 us
  transfers between devices with their start and end apart: 4, of which 4 were waited for; matrix products, arithmetic and copies ran while one was open for 1% of the time, Pallas kernels for 0%

profile of v1, /device:TPU:0, one launch (start us, length us, event | category | flops | bytes accessed | tf_op | source)
XLA Modules:
  0.0 159.0 jit_solution(3781297722359845455)
XLA Ops:
  0.6 0.0 copy-start
  0.6 0.9 reshape.50
  1.6 0.8 convert_bitcast_fusion
  2.4 0.7 copy.14
  3.1 24.6 %all-gather = bf16[16,4,4096]{2,1,0:T(4,128)(2,1)S(1)} all-gather(bf16[1,4,4096]{2,1,0:T(4,128)(2,1)S(1)} %reshape.50), channel_id=1, replica_groups=mesh['grp'=2,'lat'=16] {'lat'}, dimensions={0}, use_global_device_ids=true | all-gather | bytes 557056 | tf_op jit(solution)/shard_map/all_gather | solution.py:20
  27.8 0.1 reshape.51
  27.9 0.0 copy-start.3
  27.9 3.8 %copy.13 = bf16[32,8,2,2048]{3,1,2,0:T(8,128)(2,1)} copy(bf16[32,8,2,2048]{3,2,1,0:T(2,128)(2,1)} %bitcast.20) | data formatting | bytes 4194304
  31.7 0.0 copy-done
  31.7 0.0 copy-start.2
  31.7 0.0 copy-done.3
  31.7 0.5 convert_reduce_fusion.1
  32.2 1.1 copy-done.2
  33.3 0.5 fusion.8
  33.8 0.4 collective-permute-start
  34.2 2.3 %collective-permute-done = f32[64,4096]{1,0:T(8,128)S(1)} collective-permute-done((f32[64,4096]{1,0:T(8,128)S(1)}, f32[64,4096]{1,0:T(8,128)S(1)}, u32[]{:S(2)}, u32[]{:S(2)}) %collective-permute-start) | collective-permute-done | bytes 1048608 | tf_op jit(solution)/shard_map/ppermute | solution.py:33
  36.6 0.1 add.60
  36.7 0.1 collective-permute-start.1
  36.8 25.4 %collective-permute-done.1 = f32[64,4096]{1,0:T(8,128)S(1)} collective-permute-done((f32[64,4096]{1,0:T(8,128)S(1)}, f32[64,4096]{1,0:T(8,128)S(1)}, u32[]{:S(2)}, u32[]{:S(2)}) %collective-permute-start.1) | collective-permute-done | bytes 1048608 | tf_op jit(solution)/shard_map/ppermute | solution.py:33
  62.2 0.1 add.61
  62.3 0.0 copy-start.1
  62.3 0.1 collective-permute-start.2
  62.4 24.5 %collective-permute-done.2 = f32[64,4096]{1,0:T(8,128)S(1)} collective-permute-done((f32[64,4096]{1,0:T(8,128)S(1)}, f32[64,4096]{1,0:T(8,128)S(1)}, u32[]{:S(2)}, u32[]{:S(2)}) %collective-permute-start.2) | collective-permute-done | bytes 1048608 | tf_op jit(solution)/shard_map/ppermute | solution.py:33
  87.0 0.1 add.62
  87.1 0.1 collective-permute-start.3
  87.2 0.0 copy-done.1
  87.2 2.2 %fusion.1 = f32[256,2]{1,0:T(8,128)S(1)} fusion(bf16[256,2,2048]{2,1,0:T(2,128)(2,1)S(1)} %copy-done.1), kind=kLoop, calls=%fused_computation.5 | loop fusion | flops 3145216 | bytes 2099200 | tf_op jit(solution)/shard_map/reduce_sum | solution.py:24
  89.4 0.1 add_rsqrt_fusion
  89.6 44.7 %collective-permute-done.3 = f32[64,4096]{1,0:T(8,128)S(1)} collective-permute-done((f32[64,4096]{1,0:T(8,128)S(1)}, f32[64,4096]{1,0:T(8,128)S(1)}, u32[]{:S(2)}, u32[]{:S(2)}) %collective-permute-start.3) | collective-permute-done | bytes 1048608 | tf_op jit(solution)/shard_map/ppermute | solution.py:33
  134.2 0.1 convert_reduce_fusion
  134.4 2.7 %convolution_multiply_fusion = f32[256,4096]{1,0:T(8,128)} fusion(bf16[64,4096]{1,0:T(8,128)(2,1)S(1)} %get-tuple-element.16, f32[64,256]{1,0:T(8,128)S(1)} %get-tuple-element.22), kind=kOutput, calls=%fused_computation | convolution fusion | flops 135299072 | bytes 4784128 | tf_op jit(solution)/shard_map/dot_general | solution.py:37
  137.0 1.3 convert_reduce_fusion.2
  138.4 0.6 mul.82
  139.0 0.7 reshape.48
  139.7 2.0 %fusion = bf16[4096,256]{0,1:T(8,128)(2,1)} fusion(bf16[64,256]{1,0:T(8,128)(2,1)S(1)} %get-tuple-element.20, bf16[64,4096]{1,0:T(8,128)(2,1)S(1)} %reshape.51), kind=kOutput, calls=%fused_computation.4 | convolution fusion | flops 135266304 | bytes 2654208 | tf_op jit(solution)/shard_map/dot_general | solution.py:45
  141.7 4.1 %copy.12 = bf16[4096,256]{1,0:T(8,128)(2,1)} copy(bf16[4096,256]{0,1:T(8,128)(2,1)} %fusion) | data formatting | bytes 4194304
  145.8 6.6 %mul.74 = f32[256,2,2048]{2,1,0:T(2,128)} reshape(f32[256,4096]{1,0:T(8,128)} %convolution_multiply_fusion) | data formatting | bytes 8388608 | tf_op jit(solution)/shard_map/mul | solution.py:52
  152.3 6.7 %fusion.4 = bf16[256,2,2048]{2,1,0:T(2,128)(2,1)} fusion(f32[256,2,2048]{2,1,0:T(2,128)} %mul.74, bf16[256,2,2048]{2,1,0:T(2,128)(2,1)} %param.8, f32[256]{0:T(256)S(1)} %broadcast_multiply_fusion.1, f32[256,2]{1,0:T(8,128)S(1)} %get-tuple-element.17), kind=kLoop, calls=%fused_computation.8 | loop fusion | flops 5242880 | bytes 8391680 | tf_op jit(solution)/shard_map/convert_element_type | solution.py:54
  (6 shorter events, 0.1 us)
Async XLA Ops:
  0.6 31.1 %copy-start = (bf16[2,2048,256]{2,1,0:T(8,128)(2,1)S(1)}, bf16[2,2048,256]{2,1,0:T(8,128)(2,1)}, u32[]{:S(2)}) copy-start(bf16[2,2048,256]{2,1,0:T(8,128)(2,1)} %param.6) | copy-start | bytes 6291460
  27.9 3.8 %copy-start.3 = (f32[256]{0:T(256)S(1)}, f32[256]{0:T(256)}, u32[]{:S(2)}) copy-start(f32[256]{0:T(256)} %param.7) | copy-start | bytes 3076
  31.7 1.6 %copy-start.2 = (bf16[32,8,2,2048]{3,1,2,0:T(8,128)(2,1)S(1)}, bf16[32,8,2,2048]{3,1,2,0:T(8,128)(2,1)}, u32[]{:S(2)}) copy-start(bf16[32,8,2,2048]{3,1,2,0:T(8,128)(2,1)} %copy.13) | copy-start | bytes 6291460
  33.8 2.7 %collective-permute-start = (f32[64,4096]{1,0:T(8,128)S(1)}, f32[64,4096]{1,0:T(8,128)S(1)}, u32[]{:S(2)}, u32[]{:S(2)}) collective-permute-start(f32[64,4096]{1,0:T(8,128)S(1)} %subtract_dynamic-update-slice_fusion), channel_id=1, source_target_pairs={{0,1},{1,0},{2,3},{3,2},{4,5},{5,4},{6,7},{7,6},{8,9},{9,8},{10,11... | collective-permute-start | bytes 3145736 | tf_op jit(solution)/shard_map/ppermute | solution.py:33
  36.7 25.5 %collective-permute-start.1 = (f32[64,4096]{1,0:T(8,128)S(1)}, f32[64,4096]{1,0:T(8,128)S(1)}, u32[]{:S(2)}, u32[]{:S(2)}) collective-permute-start(f32[64,4096]{1,0:T(8,128)S(1)} %add.60), channel_id=1, source_target_pairs={{0,2},{1,3},{2,0},{3,1},{4,6},{5,7},{6,4},{7,5},{8,10},{9,11},{10,... | collective-permute-start | bytes 3145736 | tf_op jit(solution)/shard_map/ppermute | solution.py:33
  62.3 24.8 %copy-start.1 = (bf16[256,2,2048]{2,1,0:T(2,128)(2,1)S(1)}, bf16[256,2,2048]{2,1,0:T(2,128)(2,1)}, u32[]{:S(2)}) copy-start(bf16[256,2,2048]{2,1,0:T(2,128)(2,1)} %param.8) | copy-start | bytes 6291460
  62.3 24.6 %collective-permute-start.2 = (f32[64,4096]{1,0:T(8,128)S(1)}, f32[64,4096]{1,0:T(8,128)S(1)}, u32[]{:S(2)}, u32[]{:S(2)}) collective-permute-start(f32[64,4096]{1,0:T(8,128)S(1)} %add.61), channel_id=1, source_target_pairs={{0,4},{1,5},{2,6},{3,7},{4,0},{5,1},{6,2},{7,3},{8,12},{9,13},{10,... | collective-permute-start | bytes 3145736 | tf_op jit(solution)/shard_map/ppermute | solution.py:33
  87.1 47.1 %collective-permute-start.3 = (f32[64,4096]{1,0:T(8,128)S(1)}, f32[64,4096]{1,0:T(8,128)S(1)}, u32[]{:S(2)}, u32[]{:S(2)}) collective-permute-start(f32[64,4096]{1,0:T(8,128)S(1)} %add.62), channel_id=1, source_target_pairs={{0,8},{1,9},{2,10},{3,11},{4,12},{5,13},{6,14},{7,15},{8,0},{9,1},... | collective-permute-start | bytes 3145736 | tf_op jit(solution)/shard_map/ppermute | solution.py:33
